TPU v7x, 8 devices: a whole 2x2x1 slice. The times are simulated.
8 devices in a mesh: part: 1 (over z), row: 2 (over y), col: 2 (over x), dep: 2 (over core).
Axes of the slice: x: 2, y: 2, z: 1, core: 2. Of those that a mesh axis runs over, the one named last changes fastest.
Arguments:
- x_in: bfloat16 [4096, 5120], P(('part', 'row', 'col'), 'dep')
- ln_scale: float32 [5120], P('dep')
- ln_shift: float32 [5120], P('dep')
- w_up: bfloat16 [5120, 20480], P(('dep', 'row'), 'col')
- b_up: bfloat16 [20480], P('col')
- w_down: bfloat16 [20480, 5120], P(('col', 'row'), 'dep')
- b_down: bfloat16 [5120], P('dep')
- y_grad: bfloat16 [4096, 5120], P(('part', 'row', 'col'), 'dep')
Outputs:
- output 1: bfloat16 [4096, 5120], P(('part', 'row', 'col'), 'dep')
- output 2: bfloat16 [4096, 5120], P(('part', 'row', 'col'), 'dep')
- output 3: bfloat16 [5120, 20480], P(('part', 'dep', 'row'), 'col')
- output 4: float32 [20480], P(('part', 'col'))
- output 5: bfloat16 [20480, 5120], P(('part', 'col', 'row'), 'dep')
- output 6: float32 [5120], P(('part', 'dep'))
- output 7: float32 [5120], P(('part', 'dep'))
- output 8: float32 [5120], P(('part', 'dep'))
All inputs are finite; a program needn't handle non-finite values.
Results may differ from a plain program's by a relative error of at most 0.0017.
Values are sent between devices in bfloat16 or wider.
A program may use at most 1 GiB of HBM per device.

v0:
```python
import jax
import jax.numpy as jnp
from jax import lax
from jax.sharding import PartitionSpec as P

LN_EPS = 1e-5
GELU_K = 0.7978845608028654
GELU_C = 0.044715


def gelu_tanh(pre_act):
    inner_arg = GELU_K * (pre_act + GELU_C * pre_act * (pre_act * pre_act))
    return 0.5 * pre_act * (1.0 + jnp.tanh(inner_arg))


def gelu_slope(pre_act):
    squared = pre_act * pre_act
    tanh_val = jnp.tanh(GELU_K * (pre_act + GELU_C * pre_act * squared))
    return 0.5 * (1.0 + tanh_val) + 0.5 * pre_act * (1.0 - tanh_val * tanh_val) * GELU_K * (1.0 + 3.0 * GELU_C * squared)


def solution(mesh):
    dep_size = mesh.shape["dep"]
    tok_spec = P(("part", "row", "col"), "dep")
    vec_dep = P("dep")
    part_dep = P(("part", "dep"))
    in_specs = (tok_spec, vec_dep, vec_dep, P(("dep", "row"), "col"), P("col"), P(("col", "row"), "dep"), vec_dep, tok_spec)
    out_specs = (tok_spec, tok_spec, P(("part", "dep", "row"), "col"), P(("part", "col")), P(("part", "col", "row"), "dep"), part_dep, part_dep, part_dep)

    def local_step(x_in, ln_scale, ln_shift, w_up, b_up, w_down, b_down, y_grad):
        row_width = x_in.shape[1] * dep_size
        x_float = x_in.astype(jnp.float32)
        row_stats = jnp.stack([jnp.sum(x_float, axis=1), jnp.sum(x_float * x_float, axis=1)], axis=1)
        row_stats = lax.psum(row_stats, "dep")
        mean_row = row_stats[:, 0:1] / row_width
        var_row = row_stats[:, 1:2] / row_width - mean_row * mean_row
        inv_std = lax.rsqrt(var_row + LN_EPS)
        x_hat = (x_float - mean_row) * inv_std
        normed = (x_hat * ln_scale + ln_shift).astype(jnp.bfloat16)
        normed_full = lax.all_gather(normed, "col", axis=0, tiled=True)
        w_up_full = lax.all_gather(w_up, "row", axis=0, tiled=True)
        pre_part = jnp.dot(normed_full, w_up_full, preferred_element_type=jnp.float32)
        pre_act = lax.psum_scatter(pre_part, "dep", scatter_dimension=0, tiled=True) + b_up.astype(jnp.float32)
        hidden = gelu_tanh(pre_act).astype(jnp.bfloat16)
        hidden_full = lax.all_gather(hidden, "dep", axis=0, tiled=True)
        w_down_full = lax.all_gather(w_down, "row", axis=0, tiled=True)
        out_part = jnp.dot(hidden_full, w_down_full, preferred_element_type=jnp.float32)
        out_sum = lax.psum_scatter(out_part, "col", scatter_dimension=0, tiled=True)
        y_out = (x_float + out_sum + b_down.astype(jnp.float32)).astype(jnp.bfloat16)

        g_float = y_grad.astype(jnp.float32)
        grad_full = lax.all_gather(y_grad, "col", axis=0, tiled=True)
        b_down_grad = lax.psum(jnp.sum(g_float, axis=0), ("row", "col"))
        w_down_part = jnp.einsum("tf,td->fd", hidden_full, grad_full, preferred_element_type=jnp.float32)
        w_down_grad = lax.psum_scatter(w_down_part, "row", scatter_dimension=0, tiled=True).astype(jnp.bfloat16)
        hid_part = jnp.einsum("td,fd->tf", grad_full, w_down_full, preferred_element_type=jnp.float32)
        hid_grad = lax.psum_scatter(hid_part, "dep", scatter_dimension=0, tiled=True)
        pre_grad = hid_grad * gelu_slope(pre_act)
        b_up_grad = lax.psum(jnp.sum(pre_grad, axis=0), ("row", "dep"))
        pre_lowp = pre_grad.astype(jnp.bfloat16)
        pre_full = lax.all_gather(pre_lowp, "dep", axis=0, tiled=True)
        w_up_part = jnp.einsum("td,tf->df", normed_full, pre_full, preferred_element_type=jnp.float32)
        w_up_grad = lax.psum_scatter(w_up_part, "row", scatter_dimension=0, tiled=True).astype(jnp.bfloat16)
        norm_part = jnp.einsum("tf,df->td", pre_full, w_up_full, preferred_element_type=jnp.float32)
        norm_grad = lax.psum_scatter(norm_part, "col", scatter_dimension=0, tiled=True)
        value_a9 = norm_grad * ln_scale
        grad_stats = jnp.stack([jnp.sum(value_a9, axis=1), jnp.sum(value_a9 * x_hat, axis=1)], axis=1)
        grad_stats = lax.psum(grad_stats, "dep")
        x_grad = (g_float + inv_std * (value_a9 - grad_stats[:, 0:1] / row_width - x_hat * (grad_stats[:, 1:2] / row_width))).astype(jnp.bfloat16)
        gain_sums = lax.psum(jnp.stack([jnp.sum(norm_grad * x_hat, axis=0), jnp.sum(norm_grad, axis=0)]), ("row", "col"))
        return (y_out, x_grad, w_up_grad, b_up_grad, w_down_grad, b_down_grad, gain_sums[0], gain_sums[1])

    return jax.shard_map(local_step, mesh=mesh, in_specs=in_specs, out_specs=out_specs, check_vma=False)
```

profile of v0, /device:TPU:0, one launch (start us, length us, event | category | flops | bytes accessed | tf_op | source)
XLA Modules:
  0.0 4685.0 jit_solution(5643093898345617022)
XLA Ops:
  7.2 4.1 convert_reduce_fusion
  15.0 6.8 fusion.8
  23.9 127.9 %all-gather.7.cloned.1.call-done = bf16[2048,2560]{1,0:T(8,128)(2,1)} async-done(((bf16[1024,2560]{1,0:T(8,128)(2,1)}), bf16[2048,2560]{1,0:T(8,128)(2,1)}) %all-gather.7.cloned.1.call-update) | async-done | bytes 10485776 | tf_op jit(solution)/shard_map/all_gather | solution.py:40
  151.8 601.2 %all-gather.9.cloned.1.call-done = bf16[2560,10240]{1,0:T(8,128)(2,1)} async-done(((bf16[1280,10240]{1,0:T(8,128)(2,1)}), bf16[2560,10240]{1,0:T(8,128)(2,1)}) %all-gather.9.cloned.1.call-update) | async-done | bytes 52428816 | tf_op jit(solution)/shard_map/all_gather | solution.py:41
  753.0 120.6 %fusion.17 = f32[2048,10240]{1,0:T(8,128)} fusion(bf16[2048,2560]{1,0:T(8,128)(2,1)} %all-gather.7.cloned.1.call-done, bf16[2560,10240]{1,0:T(8,128)(2,1)} %all-gather.9.cloned.1.call-done), kind=kOutput, calls=%fused_computation.37 | convolution fusion | flops 107374182400 | bytes 146800640 | tf_op jit(solution)/shard_map/dot_general | solution.py:42
  873.7 8.4 all-gather.15.cloned.1.call-done
  882.1 601.0 %all-gather.13.cloned.1.call-done = bf16[10240,2560]{1,0:T(8,128)(2,1)} async-done(((bf16[5120,2560]{1,0:T(8,128)(2,1)}), bf16[10240,2560]{1,0:T(8,128)(2,1)}) %all-gather.13.cloned.1.call-update) | async-done | bytes 52428816 | tf_op jit(solution)/shard_map/all_gather | solution.py:46
  1483.1 120.5 %fusion.19 = f32[2048,10240]{1,0:T(8,128)} fusion(bf16[2048,2560]{1,0:T(8,128)(2,1)} %all-gather.15.cloned.1.call-done, bf16[10240,2560]{1,0:T(8,128)(2,1)} %all-gather.13.cloned.1.call-done), kind=kOutput, calls=%fused_computation.39 | convolution fusion | flops 107374182400 | bytes 146800640 | tf_op jit(solution)/shard_map/td,fd->tf/dot_general | solution.py:56
  1604.4 83.5 %reduce-scatter.23.cloned.1.call-done = f32[1024,10240]{1,0:T(8,128)} async-done(((f32[2048,10240]{1,0:T(8,128)}), f32[1024,10240]{1,0:T(8,128)}) %reduce-scatter.23.cloned.1.call-update) | async-done | bytes 41943056
  1687.9 50.8 %fusion.16 = (f32[10240]{0:T(1024)}, bf16[1024,10240]{1,0:T(8,128)(2,1)}, bf16[1024,10240]{1,0:T(8,128)(2,1)}) fusion(f32[1024,10240]{1,0:T(8,128)} %reduce-scatter.23.cloned.1.call-done, f32[1024,10240]{1,0:T(8,128)} %reduce-scatter.21.cloned.1.call-done, f32[10240]{0:T(1024)S(1)} %convert_element_type.35), kind=kLoop, calls=%fused_computation.36 | loop fusion | flops 230676480 | bytes 125911040 | tf_op jit(solution)/shard_map/reduce_sum | solution.py:59
  1739.5 59.1 %all-gather.17.cloned.1.call-done = bf16[2048,10240]{1,0:T(8,128)(2,1)} async-done(((bf16[1024,10240]{1,0:T(8,128)(2,1)}), bf16[2048,10240]{1,0:T(8,128)(2,1)}) %all-gather.17.cloned.1.call-update) | async-done | bytes 41943056 | tf_op jit(solution)/shard_map/all_gather | solution.py:61
  1798.6 120.4 %fusion.20 = f32[2048,2560]{1,0:T(8,128)} fusion(bf16[2048,10240]{1,0:T(8,128)(2,1)} %all-gather.17.cloned.1.call-done, bf16[2560,10240]{1,0:T(8,128)(2,1)} %all-gather.9.cloned.1.call-done), kind=kOutput, calls=%fused_computation.40 | convolution fusion | flops 107374182400 | bytes 115343360 | tf_op jit(solution)/shard_map/tf,df->td/dot_general | solution.py:64
  1919.1 120.8 %fusion.18 = f32[2048,2560]{1,0:T(8,128)} fusion(bf16[2048,10240]{1,0:T(8,128)(2,1)} %all-gather.11.cloned.1.call-done, bf16[10240,2560]{1,0:T(8,128)(2,1)} %all-gather.13.cloned.1.call-done), kind=kOutput, calls=%fused_computation.38 | convolution fusion | flops 107374182400 | bytes 115343360 | tf_op jit(solution)/shard_map/dot_general | solution.py:47
  2040.0 120.2 %fusion.21 = f32[2560,10240]{1,0:T(8,128)} fusion(bf16[2048,2560]{1,0:T(8,128)(2,1)} %all-gather.7.cloned.1.call-done, bf16[2048,10240]{1,0:T(8,128)(2,1)} %all-gather.17.cloned.1.call-done), kind=kOutput, calls=%fused_computation.41 | convolution fusion | flops 107374182400 | bytes 157286400 | tf_op jit(solution)/shard_map/td,tf->df/dot_general | solution.py:62
  2160.2 122.0 %fusion.22 = f32[10240,2560]{1,0:T(8,128)} fusion(bf16[2048,10240]{1,0:T(8,128)(2,1)} %all-gather.11.cloned.1.call-done, bf16[2048,2560]{1,0:T(8,128)(2,1)} %all-gather.15.cloned.1.call-done), kind=kOutput, calls=%fused_computation.42 | convolution fusion | flops 107374182400 | bytes 157286400 | tf_op jit(solution)/shard_map/tf,td->fd/dot_general | solution.py:54
  2283.0 13.6 psum.37
  2296.7 8.0 fusion.12
  2307.3 78.6 %reduce-scatter.17.cloned.1.call-done = f32[1024,2560]{1,0:T(8,128)} async-done(((f32[2048,2560]{1,0:T(8,128)}), f32[1024,2560]{1,0:T(8,128)}) %reduce-scatter.17.cloned.1.call-update) | async-done | bytes 10485776 | tf_op jit(solution)/shard_map/reduce_scatter | solution.py:48
  2385.8 18.9 convert_reduce_fusion.1
  2404.8 15.9 all-reduce.4
  2421.4 1097.9 %reduce-scatter.25.cloned.1.call-done = f32[1280,10240]{1,0:T(8,128)} async-done(((f32[2560,10240]{1,0:T(8,128)}), f32[1280,10240]{1,0:T(8,128)}) %reduce-scatter.25.cloned.1.call-update) | async-done | bytes 52428816
  3519.2 25.6 convert_element_type.42
  3544.8 1106.8 %reduce-scatter.27.cloned.1.call-done = f32[5120,2560]{1,0:T(8,128)} async-done(((f32[10240,2560]{1,0:T(8,128)}), f32[5120,2560]{1,0:T(8,128)}) %reduce-scatter.27.cloned.1.call-update) | async-done | bytes 52428816
  4651.6 26.4 convert_element_type.43
  (55 shorter events, 11.5 us)
Async XLA Ops:
  7.2 144.6 %all-gather.7.cloned.1.call-start = ((), (), s32[]{:S(2)}) async-start(), calls=%async_computation.6 | async-start | bytes 15728640 | tf_op jit(solution)/shard_map/all_gather | solution.py:40
  14.4 0.6 copy-start.2
  14.4 0.6 copy-start.4
  21.8 731.2 %all-gather.9.cloned.1.call-start = ((), (), s32[]{:S(2)}) async-start(), calls=%async_computation.7 | async-start | bytes 78643200 | tf_op jit(solution)/shard_map/all_gather | solution.py:41
  22.5 859.6 %all-gather.15.cloned.1.call-start = ((), (), s32[]{:S(2)}) async-start(), calls=%async_computation.11 | async-start | bytes 15728640 | tf_op jit(solution)/shard_map/all_gather | solution.py:52
  23.3 1459.9 %all-gather.13.cloned.1.call-start = ((), (), s32[]{:S(2)}) async-start(), calls=%async_computation.9 | async-start | bytes 78643200 | tf_op jit(solution)/shard_map/all_gather | solution.py:46
  23.9 1580.5 %reduce-scatter.21.cloned.1.call-start = ((), (), s32[]{:S(2)}) async-start(), calls=%async_computation.14 | async-start | bytes 125829120
  873.6 814.3 %reduce-scatter.23.cloned.1.call-start = ((), (), s32[]{:S(2)}) async-start(), calls=%async_computation.15 | async-start | bytes 125829120
  1603.7 0.7 copy-start.6
  1603.7 194.9 %all-gather.17.cloned.1.call-start = ((), (), s32[]{:S(2)}) async-start(), calls=%async_computation.12 | async-start | bytes 62914560 | tf_op jit(solution)/shard_map/all_gather | solution.py:61
  1738.7 180.4 %all-gather.11.cloned.1.call-start = ((), (), s32[]{:S(2)}) async-start(), calls=%async_computation.8 | async-start | bytes 62914560 | tf_op jit(solution)/shard_map/all_gather | solution.py:45
  1739.4 557.2 %reduce-scatter.19.cloned.1.call-start = ((), (), s32[]{:S(2)}) async-start(), calls=%async_computation.13 | async-start | bytes 31457280 | tf_op jit(solution)/shard_map/reduce_scatter | solution.py:65
  1919.0 466.9 %reduce-scatter.17.cloned.1.call-start = ((), (), s32[]{:S(2)}) async-start(), calls=%async_computation.10 | async-start | bytes 31457280 | tf_op jit(solution)/shard_map/reduce_scatter | solution.py:48
  2039.9 1479.3 %reduce-scatter.25.cloned.1.call-start = ((), (), s32[]{:S(2)}) async-start(), calls=%async_computation.16 | async-start | bytes 157286400
  2160.2 2491.4 %reduce-scatter.27.cloned.1.call-start = ((), (), s32[]{:S(2)}) async-start(), calls=%async_computation.17 | async-start | bytes 157286400
  2282.2 0.7 copy-start.7
  2282.2 0.8 copy-start
  2282.2 14.4 copy-start.1
  2282.2 14.4 copy-start.3
  2282.2 14.4 copy-start.5
Sparse Core Ops, SparseCore 0:
  21.9 129.8 all-gather.6
  153.3 599.6 all-gather.8
  754.5 127.5 all-gather.14
  883.5 599.6 all-gather.12
  1485.3 84.0 reduce-scatter.20
  1603.8 84.0 reduce-scatter.22
  1738.8 59.7 all-gather.16
  1800.7 59.7 all-gather.10
  1919.1 232.5 reduce-scatter.18
  2154.4 231.3 reduce-scatter.16
  2388.1 1131.0 reduce-scatter.24
  3521.3 1130.2 reduce-scatter.26
where the time goes:
time: 4690 us
  waiting for transfers between devices  3770 us (80%)
  matrix products  724 us (15%)
  other arithmetic  141 us (3%)
    unnamed x16, waiting for transfers between devices  2290 us
    all_gather x1, waiting for transfers between devices, local_step(): w_up_full = lax.all_gather(w_up, 'row', axis=0, tiled=True)  601 us
    all_gather x1, waiting for transfers between devices, local_step(): w_down_full = lax.all_gather(w_down, 'row', axis=0, tiled=True)  601 us
    all_gather x1, waiting for transfers between devices, local_step(): normed_full = lax.all_gather(normed, 'col', axis=0, tiled=True)  128 us
    dot_general x1, matrix products, local_step(): jnp.einsum('tf,td->fd', hidden_full, grad_full, preferred_element_type=jn...  122 us
    dot_general x1, matrix products, local_step(): jnp.dot(hidden_full, w_down_full, preferred_element_type=jnp.float32)  121 us
    dot_general x1, matrix products, local_step(): jnp.dot(normed_full, w_up_full, preferred_element_type=jnp.float32)  121 us
    dot_general x1, matrix products, local_step(): jnp.einsum('td,fd->tf', grad_full, w_down_full, preferred_element_type=jn...  121 us
  transfers between devices with their start and end apart: 12, of which 9 were waited for; matrix products, arithmetic and copies ran while one was open for 17% of the time, Pallas kernels for 0%

commit v1 on v0

v1 whole, which is shorter than its diff:
```python
import jax
import jax.numpy as jnp
from jax import lax
from jax.sharding import PartitionSpec as P


LN_EPS = 1e-5
GELU_K = 0.7978845608028654
GELU_C = 0.044715
SWAP = ((0, 1), (1, 0))
F32 = jnp.float32
BF16 = jnp.bfloat16


def gelu_tanh(pre_act):
    inner_arg = GELU_K * (pre_act + GELU_C * pre_act * (pre_act * pre_act))
    return 0.5 * pre_act * (1.0 + jnp.tanh(inner_arg))


def gelu_slope(pre_act):
    squared = pre_act * pre_act
    tanh_val = jnp.tanh(GELU_K * (pre_act + GELU_C * pre_act * squared))
    return 0.5 * (1.0 + tanh_val) + 0.5 * pre_act * (1.0 - tanh_val * tanh_val) * GELU_K * (1.0 + 3.0 * GELU_C * squared)


def swap(val, axis):
    return lax.ppermute(val, axis, SWAP)


def ordered(idx, mine, other, axis):
    return jnp.where(idx == 0, jnp.concatenate([mine, other], axis), jnp.concatenate([other, mine], axis))


def dot_nn(lhs, rhs):
    return lax.dot_general(lhs, rhs, (((1,), (0,)), ((), ())), preferred_element_type=F32)


def dot_nt(lhs, rhs):
    return lax.dot_general(lhs, rhs, (((1,), (1,)), ((), ())), preferred_element_type=F32)


def dot_tn(lhs, rhs):
    return lax.dot_general(lhs, rhs, (((0,), (0,)), ((), ())), preferred_element_type=F32)


def solution(mesh):
    assert mesh.shape["row"] == 2 and mesh.shape["col"] == 2 and mesh.shape["dep"] == 2
    tok_spec = P(("part", "row", "col"), "dep")
    vec_dep = P("dep")
    part_dep = P(("part", "dep"))
    in_specs = (tok_spec, vec_dep, vec_dep, P(("dep", "row"), "col"), P("col"), P(("col", "row"), "dep"), vec_dep, tok_spec)
    out_specs = (tok_spec, tok_spec, P(("part", "dep", "row"), "col"), P(("part", "col")), P(("part", "col", "row"), "dep"), part_dep, part_dep, part_dep)

    def layer(x_in, ln_scale, ln_shift, w_up, b_up, w_down, b_down, y_grad):
        row = lax.axis_index("row")
        dep = lax.axis_index("dep")
        half_d = x_in.shape[1]
        row_width = half_d * 2
        quarter = w_up.shape[1] // 2
        own_f = quarter // 2
        up_rows = w_up.shape[0]

        last = [None]

        def after(vals):
            if last[0] is None:
                return vals
            return lax.optimization_barrier((vals, last[0]))[0]

        def step(fn, *vals):
            out = fn(*after(vals))
            last[0] = out[0] if isinstance(out, tuple) else out
            return out

        def launch(val, axis):
            val = after(val)
            return lax.ppermute(val, axis, SWAP)

        a_mine, a_peer, g_mine, g_peer = {}, {}, {}, {}
        hid_grad, pre_half, pre, hidden, pre_grad, pre_lowp = {}, {}, {}, {}, {}, {}
        out_came, out_chip, norm_came, norm_chip = {}, {}, {}, {}
        far_at = (0, (1 - row) * quarter + (1 - dep) * own_f)
        near_at = (0, (1 - row) * quarter + dep * own_f)
        pass_at = (0, row * quarter + (1 - dep) * own_f)
        keep_at = (0, row * quarter + dep * own_f)
        up_block = (up_rows, own_f)

        g_mine["O"] = y_grad
        g_mine["X"] = launch(y_grad, "col")
        up_far = launch(step(lambda w: lax.dynamic_slice(w, far_at, up_block), w_up), "row")

        def stats_of(x):
            x_float = x.astype(F32)
            return jnp.stack([jnp.sum(x_float, axis=1), jnp.sum(x_float * x_float, axis=1)], axis=0)

        row_stats = step(stats_of, x_in)
        row_stats = row_stats + swap(row_stats, "dep")
        mean_row = (row_stats[0] / row_width)[:, None]
        var_row = (row_stats[1] / row_width)[:, None] - mean_row * mean_row
        inv_std = lax.rsqrt(var_row + LN_EPS)
        normed = step(lambda x, m, i: ((x.astype(F32) - m) * i * ln_scale + ln_shift).astype(BF16), x_in, mean_row, inv_std)
        a_mine["O"] = normed
        a_mine["Y"] = launch(normed, "row")
        a_mine["X"] = launch(normed, "col")
        up_near = launch(step(lambda w: lax.dynamic_slice(w, near_at, up_block), w_up), "row")
        g_peer["O"] = launch(y_grad, "dep")
        down_peer = launch(step(lambda w: lax.dynamic_slice(w, ((1 - dep) * own_f, 0), (own_f, half_d)), w_down), "dep")
        up_pass = launch(step(lambda w: lax.dynamic_slice(w, pass_at, up_block), w_up), "dep")
        a_peer["O"] = launch(normed, "dep")
        down_own = step(lambda w: lax.dynamic_slice(w, (dep * own_f, 0), (own_f, half_d)), w_down)
        bias = lax.dynamic_slice(b_up, (row * quarter + dep * own_f,), (own_f,)).astype(F32)

        def run_hid_grad(k):
            part = step(dot_nt, g_mine[k], down_own)
            hid_grad[k] = step(lambda g, w, p: dot_nt(g, w) + p, g_peer[k], down_peer, part)

        def run_pre_half(k):
            pre_half[k] = step(dot_nn, a_peer[k], up_peer)

        def run_pre(k):
            def body(act, weight, half):
                total = dot_nn(act, weight) + half + bias
                return gelu_tanh(total).astype(BF16), total

            hidden[k], pre[k] = step(body, a_mine[k], up_own, pre_half[k])

        def run_pre_grad(k):
            def body(grad, act):
                full = grad * gelu_slope(act)
                return full.astype(BF16), full

            pre_lowp[k], pre_grad[k] = step(body, hid_grad[k], pre[k])

        def out_peer(k):
            out_came[k] = launch(step(dot_nn, hidden[k], down_peer), "dep")

        def out_own(k):
            out_chip[k] = step(lambda h, w, c: dot_nn(h, w) + c, hidden[k], down_own, out_came[k])

        def norm_peer(k):
            norm_came[k] = launch(step(dot_nt, pre_lowp[k], up_peer), "dep")

        def norm_own(k):
            norm_chip[k] = step(lambda h, w, c: dot_nt(h, w) + c, pre_lowp[k], up_own, norm_came[k])

        run_hid_grad("O")
        g_peer["X"] = launch(g_mine["X"], "dep")
        run_hid_grad("X")
        far_here = launch(up_far, "dep")
        up_peer = step(lambda kept, came: ordered(row, kept, came, 0), up_pass, far_here)
        run_pre_half("O")
        a_peer["X"] = launch(a_mine["X"], "dep")
        run_pre_half("X")
        a_peer["Y"] = launch(a_mine["Y"], "dep")
        a_mine["D"] = launch(a_mine["Y"], "col")
        run_pre_half("Y")
        a_peer["D"] = launch(a_mine["D"], "dep")
        run_pre_half("D")
        up_own = step(lambda w, came: ordered(row, lax.dynamic_slice(w, keep_at, up_block), came, 0), w_up, up_near)
        g_mine["Y"] = launch(y_grad, "row")
        g_mine["D"] = launch(g_mine["X"], "row")
        run_pre("D")
        out_peer("D")
        run_pre("Y")
        out_peer("Y")
        out_own("D")
        out_diag = launch(out_chip["D"], "col")
        out_own("Y")
        run_pre("X")
        run_pre("O")
        out_peer("X")
        out_peer("O")
        g_peer["Y"] = launch(g_mine["Y"], "dep")
        run_pre_grad("X")
        run_pre_grad("O")
        out_own("O")
        run_hid_grad("Y")
        g_peer["D"] = launch(g_mine["D"], "dep")
        run_pre_grad("Y")
        norm_peer("Y")
        run_hid_grad("D")
        run_pre_grad("D")
        norm_peer("D")
        b_up_own = step(lambda p: sum(jnp.sum(v, axis=0) for v in p.values()), pre_grad)
        b_up_came = launch(b_up_own, "dep")
        norm_own("Y")
        b_up_near = step(lambda own, came: ordered(dep, own, came, 0), b_up_own, b_up_came)
        b_up_far = launch(b_up_near, "row")
        norm_peer("X")
        norm_own("D")
        norm_diag = launch(norm_chip["D"], "col")
        out_own("X")
        out_x = launch(out_chip["X"], "col")
        out_y = launch(step(jnp.add, out_chip["Y"], out_diag), "row")
        norm_own("X")
        norm_x = launch(norm_chip["X"], "col")
        norm_peer("O")

        def token_sum(lhs, rhs):
            total = step(dot_tn, lhs["O"], rhs["O"])
            for k in "XY":
                total = step(lambda a, b, t: dot_tn(a, b) + t, lhs[k], rhs[k], total)
            return step(lambda a, b, t: (dot_tn(a, b) + t).astype(BF16), lhs["D"], rhs["D"], total)

        down_g_came = launch(token_sum(hidden, g_peer), "dep")
        norm_own("O")
        down_g_own = token_sum(hidden, g_mine)
        norm_y = launch(step(jnp.add, norm_chip["Y"], norm_diag), "row")
        up_g_came = launch(token_sum(a_peer, pre_lowp), "dep")
        up_g_own = token_sum(a_mine, pre_lowp)

        def up_rows_of(own, came, row_idx):
            at = (row_idx * up_rows, 0)
            return ordered(dep, lax.dynamic_slice(own, at, up_block), lax.dynamic_slice(came, at, up_block), 1)

        up_g_far = launch(step(lambda own, came: up_rows_of(own, came, 1 - row), up_g_own, up_g_came), "row")
        up_g_near = step(lambda own, came: up_rows_of(own, came, row), up_g_own, up_g_came)
        w_down_grad = step(lambda own, came: ordered(dep, own, came, 0), down_g_own, down_g_came)
        x_float = x_in.astype(F32)
        y_out = step(lambda x, c, n, y: (x.astype(F32) + ((c + n) + y) + b_down.astype(F32)).astype(BF16), x_in, out_chip["O"], out_x, out_y)
        norm_grad = step(lambda c, n, y: (c + n) + y, norm_chip["O"], norm_x, norm_y)
        w_up_grad = ordered(row, up_g_near, up_g_far, 1)

        b_up_grad = ordered(row, b_up_near, b_up_far, 0)
        g_float = y_grad.astype(F32)
        b_down_grad = sum(jnp.sum(g.astype(F32), axis=0) for g in g_mine.values())

        x_hat = (x_float - mean_row) * inv_std
        value = norm_grad * ln_scale
        grad_stats = jnp.stack([jnp.sum(value, axis=1), jnp.sum(value * x_hat, axis=1)], axis=0)
        grad_stats = grad_stats + swap(grad_stats, "dep")
        mean_one = (grad_stats[0] / row_width)[:, None]
        mean_two = (grad_stats[1] / row_width)[:, None]
        x_grad = (g_float + inv_std * (value - mean_one - x_hat * mean_two)).astype(BF16)
        gain_sums = jnp.stack([jnp.sum(norm_grad * x_hat, axis=0), jnp.sum(norm_grad, axis=0)])
        gain_sums = gain_sums + swap(gain_sums, "col")
        gain_sums = gain_sums + swap(gain_sums, "row")
        return (y_out, x_grad, w_up_grad, b_up_grad, w_down_grad, b_down_grad, gain_sums[0], gain_sums[1])

    mapped = jax.shard_map(layer, mesh=mesh, in_specs=in_specs, out_specs=out_specs, check_vma=False)

    def run(*args):
        jax.eval_shape(mapped, *args)
        return mapped(*args)

    return run
```

time: 4690 us -> 2630 us (0.56)
  waiting for transfers between devices: 3770 us -> 1200 us
  matrix products: 724 us -> 1070 us
  other arithmetic: 141 us -> 262 us
  local copies, waits for them, and re-layouts: 2.66 us -> 55.8 us
    unnamed x16 -> x0, waiting for transfers between devices: 2290 us -> none
    all_gather x6 -> x0, waiting for transfers between devices: 1400 us -> none  [the longest x1 601 us: local_step(): w_up_full = lax.all_gather(w_up, 'row', axis=0, tiled=True)]
    ppermute x0 -> x42, waiting for transfers between devices: none -> 1200 us  [the longest x38 950 us: launch(): return lax.ppermute(val, axis, SWAP)]
    dot_general x6 -> x48, matrix products: 724 us -> 1070 us  [the longest x16 397 us: dot_tn(): lax.dot_general(lhs, rhs, (((0,), (0,)), ((), ())), preferred_element_typ...]
    select_n x0 -> x8, other arithmetic: none -> 95.7 us  [ordered(): jnp.where(idx == 0, jnp.concatenate([mine, other], axis), jnp.concatenate...]
    reduce_scatter x2 -> x0, waiting for transfers between devices: 78.6 us -> none  [the longest x1 78.6 us: local_step(): out_sum = lax.psum_scatter(out_part, 'col', scatter_dimension=0, tiled=True)]
    dynamic_slice x0 -> x9, local copies, waits for them, and re-layouts: none -> 54.9 us  [the longest x1 10.9 us: layer(): lax.dynamic_slice(w, ((1 - dep) * own_f, 0), (own_f, half_d))]
  transfers between devices with their start and end apart: 12 -> 42, of which waited for: 9 -> 19; matrix products, arithmetic and copies ran while one was open for 17% -> 39% of each run, Pallas kernels for 0% -> 0%
where the time goes in v1:
time: 2630 us; the launch traced here: 2620 us
  waiting for transfers between devices  1200 us (46%)
  matrix products  1070 us (41%)
  other arithmetic  262 us (10%)
  local copies, waits for them, and re-layouts  55.8 us (2%)
  starting transfers between devices  29.1 us (1%)
    ppermute x38, waiting for transfers between devices, launch(): return lax.ppermute(val, axis, SWAP)  950 us
    dot_general x16, matrix products, dot_tn(): lax.dot_general(lhs, rhs, (((0,), (0,)), ((), ())), preferred_element_typ...  397 us
    dot_general x16, matrix products, dot_nt(): lax.dot_general(lhs, rhs, (((1,), (1,)), ((), ())), preferred_element_typ...  343 us
    dot_general x16, matrix products, dot_nn(): lax.dot_general(lhs, rhs, (((1,), (0,)), ((), ())), preferred_element_typ...  332 us
    ppermute x4, waiting for transfers between devices, swap(): return lax.ppermute(val, axis, SWAP)  255 us
    select_n x8, other arithmetic, ordered(): jnp.where(idx == 0, jnp.concatenate([mine, other], axis), jnp.concatenate...  95.7 us
    convert_element_type x4, other arithmetic, body(): return (full.astype(BF16), full)  58.9 us
  transfers between devices with their start and end apart: 42, of which 19 were waited for; matrix products, arithmetic and copies ran while one was open for 39% of the time, Pallas kernels for 0%

profile of v1, /device:TPU:0, one launch (start us, length us, event | category | flops | bytes accessed | tf_op | source)
XLA Modules:
  0.0 2624.6 jit_solution(10101530589226540690)
XLA Ops:
  97.1 54.2 %collective-permute-done.7 = bf16[1024,2560]{1,0:T(8,128)(2,1)} collective-permute-done((bf16[1024,2560]{1,0:T(8,128)(2,1)}, bf16[1024,2560]{1,0:T(8,128)(2,1)}, u32[]{:S(2)}, u32[]{:S(2)}) %collective-permute-start.7) | collective-permute-done | bytes 5242912 | tf_op jit(solution)/shard_map/ppermute | solution.py:77
  196.4 98.8 %collective-permute-done.6 = bf16[1280,2560]{1,0:T(8,128)(2,1)} collective-permute-done((bf16[1280,2560]{1,0:T(8,128)(2,1)}, bf16[1280,2560]{1,0:T(8,128)(2,1)}, u32[]{:S(2)}, u32[]{:S(2)}) %collective-permute-start.6) | collective-permute-done | bytes 6553632 | tf_op jit(solution)/shard_map/ppermute | solution.py:77
  337.1 73.8 %collective-permute-done.3 = bf16[1024,2560]{1,0:T(8,128)(2,1)S(1)} collective-permute-done((bf16[1024,2560]{1,0:T(8,128)(2,1)}, bf16[1024,2560]{1,0:T(8,128)(2,1)S(1)}, u32[]{:S(2)}, u32[]{:S(2)}) %collective-permute-start.3) | collective-permute-done | bytes 5242912 | tf_op jit(solution)/shard_map/ppermute | solution.py:77
  437.3 89.1 %collective-permute-done.2 = bf16[1024,2560]{1,0:T(8,128)(2,1)} collective-permute-done((bf16[1024,2560]{1,0:T(8,128)(2,1)S(1)}, bf16[1024,2560]{1,0:T(8,128)(2,1)}, u32[]{:S(2)}, u32[]{:S(2)}) %collective-permute-start.2) | collective-permute-done | bytes 5242912 | tf_op jit(solution)/shard_map/ppermute | solution.py:77
  551.9 90.3 %collective-permute-done.13 = bf16[1024,2560]{1,0:T(8,128)(2,1)} collective-permute-done((bf16[1024,2560]{1,0:T(8,128)(2,1)}, bf16[1024,2560]{1,0:T(8,128)(2,1)}, u32[]{:S(2)}, u32[]{:S(2)}) %collective-permute-start.13) | collective-permute-done | bytes 5242912 | tf_op jit(solution)/shard_map/ppermute | solution.py:77
  671.8 114.3 %collective-permute-done.1 = bf16[1280,2560]{1,0:T(8,128)(2,1)} collective-permute-done((bf16[1280,2560]{1,0:T(8,128)(2,1)}, bf16[1280,2560]{1,0:T(8,128)(2,1)}, u32[]{:S(2)}, u32[]{:S(2)}) %collective-permute-start.1) | collective-permute-done | bytes 6553632 | tf_op jit(solution)/shard_map/ppermute | solution.py:77
  804.6 24.1 multiply_convert_fusion.3
  849.7 25.2 multiply_convert_fusion.2
  933.9 24.9 multiply_convert_fusion.1
  958.8 23.5 multiply_convert_fusion
  1041.1 97.5 %collective-permute-done.21 = bf16[1024,2560]{1,0:T(8,128)(2,1)} collective-permute-done((bf16[1024,2560]{1,0:T(8,128)(2,1)}, bf16[1024,2560]{1,0:T(8,128)(2,1)}, u32[]{:S(2)}, u32[]{:S(2)}) %collective-permute-start.21) | collective-permute-done | bytes 5242912 | tf_op jit(solution)/shard_map/ppermute | solution.py:77
  1537.3 25.1 convolution_add_fusion.7
  1562.4 28.5 %convolution_add_fusion.6 = f32[2560,2560]{1,0:T(8,128)} fusion(f32[2560,2560]{1,0:T(8,128)} %convolution_add_fusion.7, bf16[1024,2560]{1,0:T(8,128)(2,1)} %get-tuple-element.362, bf16[1024,2560]{1,0:T(8,128)(2,1)} %collective-permute-done.22), kind=kOutput, calls=%fused_computation.12 | convolution fusion | flops 13428326400 | bytes 62914560 | tf_op jit(solution)/shard_map/dot_general | solution.py:43
  1657.0 28.8 %convolution_add_fusion.5 = f32[2560,2560]{1,0:T(8,128)} fusion(f32[2560,2560]{1,0:T(8,128)} %fusion.29, bf16[1024,2560]{1,0:T(8,128)(2,1)} %get-tuple-element.359, bf16[1024,2560]{1,0:T(8,128)(2,1)} %collective-permute-done.7), kind=kOutput, calls=%fused_computation.11 | convolution fusion | flops 13428326400 | bytes 62914560 | tf_op jit(solution)/shard_map/dot_general | solution.py:43
  1685.8 28.5 %convolution_add_fusion.4 = f32[2560,2560]{1,0:T(8,128)} fusion(f32[2560,2560]{1,0:T(8,128)} %convolution_add_fusion.5, bf16[1024,2560]{1,0:T(8,128)(2,1)} %get-tuple-element.362, bf16[1024,2560]{1,0:T(8,128)(2,1)} %collective-permute-done.21), kind=kOutput, calls=%fused_computation.10 | convolution fusion | flops 13428326400 | bytes 62914560 | tf_op jit(solution)/shard_map/dot_general | solution.py:43
  1771.6 26.6 %convolution_add_fusion.3 = f32[2560,2560]{1,0:T(8,128)} fusion(f32[2560,2560]{1,0:T(8,128)} %fusion.30, bf16[1024,2560]{1,0:T(8,128)(2,1)} %collective-permute-done.12, bf16[1024,2560]{1,0:T(8,128)(2,1)S(1)} %bitcast.124), kind=kOutput, calls=%fused_computation.9 | convolution fusion | flops 13428326400 | bytes 62914560 | tf_op jit(solution)/shard_map/dot_general | solution.py:43
  1798.2 28.9 %convolution_add_fusion.2 = f32[2560,2560]{1,0:T(8,128)} fusion(f32[2560,2560]{1,0:T(8,128)} %convolution_add_fusion.3, bf16[1024,2560]{1,0:T(8,128)(2,1)} %copy-done.18, bf16[1024,2560]{1,0:T(8,128)(2,1)} %copy-done.2), kind=kOutput, calls=%fused_computation.8 | convolution fusion | flops 13428326400 | bytes 62914560 | tf_op jit(solution)/shard_map/dot_general | solution.py:43
  1888.0 26.7 %convolution_add_fusion.1 = f32[2560,2560]{1,0:T(8,128)} fusion(f32[2560,2560]{1,0:T(8,128)} %fusion.31, bf16[1024,2560]{1,0:T(8,128)(2,1)} %copy-done.17, bf16[1024,2560]{1,0:T(8,128)(2,1)S(1)} %bitcast.124), kind=kOutput, calls=%fused_computation.7 | convolution fusion | flops 13428326400 | bytes 62914560 | tf_op jit(solution)/shard_map/dot_general | solution.py:43
  1914.6 28.8 %convolution_add_fusion = f32[2560,2560]{1,0:T(8,128)} fusion(f32[2560,2560]{1,0:T(8,128)} %convolution_add_fusion.1, bf16[1024,2560]{1,0:T(8,128)(2,1)} %collective-permute-done.2, bf16[1024,2560]{1,0:T(8,128)(2,1)} %copy-done.2), kind=kOutput, calls=%fused_computation.6 | convolution fusion | flops 13428326400 | bytes 62914560 | tf_op jit(solution)/shard_map/dot_general | solution.py:43
  1992.9 27.3 %maximum_select_fusion = bf16[5120,2560]{1,0:T(8,128)(2,1)} fusion(bf16[2560,2560]{1,0:T(8,128)(2,1)} %collective-permute-done.32, bf16[2560,2560]{1,0:T(8,128)(2,1)} %add_convert_fusion.2, pred[]{:T(512)S(6)} %eq.5), kind=kLoop, calls=%fused_computation | loop fusion | flops 117964800 | bytes 52428800 | tf_op jit(solution)/shard_map/jit(_where)/select_n | solution.py:31
  2020.3 72.6 %collective-permute-done.29 = f32[1024,2560]{1,0:T(8,128)} collective-permute-done((f32[1024,2560]{1,0:T(8,128)}, f32[1024,2560]{1,0:T(8,128)}, u32[]{:S(2)}, u32[]{:S(2)}) %collective-permute-start.29) | collective-permute-done | bytes 10485792 | tf_op jit(solution)/shard_map/ppermute | solution.py:77
  2108.9 207.8 %collective-permute-done.35 = f32[1024,2560]{1,0:T(8,128)} collective-permute-done((f32[1024,2560]{1,0:T(8,128)}, f32[1024,2560]{1,0:T(8,128)}, u32[]{:S(2)}, u32[]{:S(2)}) %collective-permute-start.35) | collective-permute-done | bytes 10485792 | tf_op jit(solution)/shard_map/ppermute | solution.py:77
  2343.8 253.9 %collective-permute-done.41 = f32[2,2560]{1,0:T(2,128)S(1)} collective-permute-done((f32[2,2560]{1,0:T(2,128)S(1)}, f32[2,2560]{1,0:T(2,128)S(1)}, u32[]{:S(2)}, u32[]{:S(2)}) %collective-permute-start.41) | collective-permute-done | bytes 20512 | tf_op jit(solution)/shard_map/ppermute | solution.py:27
  2598.4 26.0 maximum_select_fusion.1
  (271 shorter events, 1098.0 us)
Async XLA Ops:
  34.8 116.5 %collective-permute-start.7 = (bf16[1024,2560]{1,0:T(8,128)(2,1)}, bf16[1024,2560]{1,0:T(8,128)(2,1)}, u32[]{:S(2)}, u32[]{:S(2)}) collective-permute-start(bf16[1024,2560]{1,0:T(8,128)(2,1)} %param.15), channel_id=1, source_target_pairs={{0,2},{2,0},{1,3},{3,1},{4,6},{6,4},{5,7},{7,5}} | collective-permute-start | bytes 15728648 | tf_op jit(solution)/shard_map/ppermute | solution.py:77
  151.3 143.9 %collective-permute-start.6 = (bf16[1280,2560]{1,0:T(8,128)(2,1)}, bf16[1280,2560]{1,0:T(8,128)(2,1)}, u32[]{:S(2)}, u32[]{:S(2)}) collective-permute-start(bf16[1280,2560]{1,0:T(8,128)(2,1)} %constant_dynamic-slice_fusion.9), channel_id=1, source_target_pairs={{0,4},{4,0},{1,5},{5,1},{2,6},{6,2},{3,7},{7,3}} | collective-permute-start | bytes 19660808 | tf_op jit(solution)/shard_map/ppermute | solution.py:77
  153.1 144.3 %collective-permute-start.5 = (bf16[1280,2560]{1,0:T(8,128)(2,1)}, bf16[1280,2560]{1,0:T(8,128)(2,1)}, u32[]{:S(2)}, u32[]{:S(2)}) collective-permute-start(bf16[1280,2560]{1,0:T(8,128)(2,1)} %constant_dynamic-slice_fusion.6), channel_id=1, source_target_pairs={{0,1},{1,0},{2,3},{3,2},{4,5},{5,4},{6,7},{7,6}} | collective-permute-start | bytes 19660808 | tf_op jit(solution)/shard_map/ppermute | solution.py:77
  295.7 115.2 %collective-permute-start.3 = (bf16[1024,2560]{1,0:T(8,128)(2,1)}, bf16[1024,2560]{1,0:T(8,128)(2,1)S(1)}, u32[]{:S(2)}, u32[]{:S(2)}) collective-permute-start(bf16[1024,2560]{1,0:T(8,128)(2,1)} %add_convert_fusion.5), channel_id=1, source_target_pairs={{0,2},{2,0},{1,3},{3,1},{4,6},{6,4},{5,7},{7,5}} | collective-permute-start | bytes 15728648 | tf_op jit(solution)/shard_map/ppermute | solution.py:77
  410.9 115.5 %collective-permute-start.2 = (bf16[1024,2560]{1,0:T(8,128)(2,1)S(1)}, bf16[1024,2560]{1,0:T(8,128)(2,1)}, u32[]{:S(2)}, u32[]{:S(2)}) collective-permute-start(bf16[1024,2560]{1,0:T(8,128)(2,1)S(1)} %bitcast.130), channel_id=1, source_target_pairs={{0,4},{4,0},{1,5},{5,1},{2,6},{6,2},{3,7},{7,3}} | collective-permute-start | bytes 15728648 | tf_op jit(solution)/shard_map/ppermute | solution.py:77
  526.5 115.8 %collective-permute-start.13 = (bf16[1024,2560]{1,0:T(8,128)(2,1)}, bf16[1024,2560]{1,0:T(8,128)(2,1)}, u32[]{:S(2)}, u32[]{:S(2)}) collective-permute-start(bf16[1024,2560]{1,0:T(8,128)(2,1)} %collective-permute-done.2), channel_id=1, source_target_pairs={{0,2},{2,0},{1,3},{3,1},{4,6},{6,4},{5,7},{7,5}} | collective-permute-start | bytes 15728648 | tf_op jit(solution)/shard_map/ppermute | solution.py:77
  642.2 143.9 %collective-permute-start.1 = (bf16[1280,2560]{1,0:T(8,128)(2,1)}, bf16[1280,2560]{1,0:T(8,128)(2,1)}, u32[]{:S(2)}, u32[]{:S(2)}) collective-permute-start(bf16[1280,2560]{1,0:T(8,128)(2,1)} %constant_dynamic-slice_fusion.8), channel_id=1, source_target_pairs={{0,4},{4,0},{1,5},{5,1},{2,6},{6,2},{3,7},{7,3}} | collective-permute-start | bytes 19660808 | tf_op jit(solution)/shard_map/ppermute | solution.py:77
  1022.3 131.5 %collective-permute-start.18 = (f32[1024,2560]{1,0:T(8,128)}, f32[1024,2560]{1,0:T(8,128)}, u32[]{:S(2)}, u32[]{:S(2)}) collective-permute-start(f32[1024,2560]{1,0:T(8,128)} %fusion.21), channel_id=1, source_target_pairs={{0,1},{1,0},{2,3},{3,2},{4,5},{5,4},{6,7},{7,6}} | collective-permute-start | bytes 31457288 | tf_op jit(solution)/shard_map/ppermute | solution.py:77
  1022.3 116.2 %collective-permute-start.21 = (bf16[1024,2560]{1,0:T(8,128)(2,1)}, bf16[1024,2560]{1,0:T(8,128)(2,1)}, u32[]{:S(2)}, u32[]{:S(2)}) collective-permute-start(bf16[1024,2560]{1,0:T(8,128)(2,1)} %param.15), channel_id=1, source_target_pairs={{0,4},{4,0},{1,5},{5,1},{2,6},{6,2},{3,7},{7,3}} | collective-permute-start | bytes 15728648 | tf_op jit(solution)/shard_map/ppermute | solution.py:77
  1024.0 226.4 %collective-permute-start.20 = (bf16[1024,2560]{1,0:T(8,128)(2,1)}, bf16[1024,2560]{1,0:T(8,128)(2,1)}, u32[]{:S(2)}, u32[]{:S(2)}) collective-permute-start(bf16[1024,2560]{1,0:T(8,128)(2,1)} %collective-permute-done.7), channel_id=1, source_target_pairs={{0,4},{4,0},{1,5},{5,1},{2,6},{6,2},{3,7},{7,3}} | collective-permute-start | bytes 15728648 | tf_op jit(solution)/shard_map/ppermute | solution.py:77
  1138.5 295.6 %collective-permute-start.19 = (f32[1024,2560]{1,0:T(8,128)}, f32[1024,2560]{1,0:T(8,128)}, u32[]{:S(2)}, u32[]{:S(2)}) collective-permute-start(f32[1024,2560]{1,0:T(8,128)} %fusion.20), channel_id=1, source_target_pairs={{0,1},{1,0},{2,3},{3,2},{4,5},{5,4},{6,7},{7,6}} | collective-permute-start | bytes 31457288 | tf_op jit(solution)/shard_map/ppermute | solution.py:77
  1139.0 317.6 %collective-permute-start.28 = (f32[1024,2560]{1,0:T(8,128)}, f32[1024,2560]{1,0:T(8,128)}, u32[]{:S(2)}, u32[]{:S(2)}) collective-permute-start(f32[1024,2560]{1,0:T(8,128)} %convolution_add_fusion.17), channel_id=1, source_target_pairs={{0,2},{2,0},{1,3},{3,1},{4,6},{6,4},{5,7},{7,5}} | collective-permute-start | bytes 31457288 | tf_op jit(solution)/shard_map/ppermute | solution.py:77
  1269.6 97.7 %collective-permute-start.26 = (f32[1024,2560]{1,0:T(8,128)}, f32[1024,2560]{1,0:T(8,128)}, u32[]{:S(2)}, u32[]{:S(2)}) collective-permute-start(f32[1024,2560]{1,0:T(8,128)} %fusion.23), channel_id=1, source_target_pairs={{0,1},{1,0},{2,3},{3,2},{4,5},{5,4},{6,7},{7,6}} | collective-permute-start | bytes 31457288 | tf_op jit(solution)/shard_map/ppermute | solution.py:77
  1410.8 60.9 %collective-permute-start.30 = (f32[1024,2560]{1,0:T(8,128)}, f32[1024,2560]{1,0:T(8,128)}, u32[]{:S(2)}, u32[]{:S(2)}) collective-permute-start(f32[1024,2560]{1,0:T(8,128)} %fusion.26), channel_id=1, source_target_pairs={{0,1},{1,0},{2,3},{3,2},{4,5},{5,4},{6,7},{7,6}} | collective-permute-start | bytes 31457288 | tf_op jit(solution)/shard_map/ppermute | solution.py:77
  1456.7 279.0 %collective-permute-start.33 = (f32[1024,2560]{1,0:T(8,128)}, f32[1024,2560]{1,0:T(8,128)}, u32[]{:S(2)}, u32[]{:S(2)}) collective-permute-start(f32[1024,2560]{1,0:T(8,128)} %convolution_add_fusion.11), channel_id=1, source_target_pairs={{0,2},{2,0},{1,3},{3,1},{4,6},{6,4},{5,7},{7,5}} | collective-permute-start | bytes 31457288 | tf_op jit(solution)/shard_map/ppermute | solution.py:77
  1514.8 97.3 %collective-permute-start.31 = (f32[1024,2560]{1,0:T(8,128)}, f32[1024,2560]{1,0:T(8,128)}, u32[]{:S(2)}, u32[]{:S(2)}) collective-permute-start(f32[1024,2560]{1,0:T(8,128)} %fusion.27), channel_id=1, source_target_pairs={{0,1},{1,0},{2,3},{3,2},{4,5},{5,4},{6,7},{7,6}} | collective-permute-start | bytes 31457288 | tf_op jit(solution)/shard_map/ppermute | solution.py:77
  1850.0 114.7 %collective-permute-start.34 = (bf16[2560,2560]{1,0:T(8,128)(2,1)}, bf16[2560,2560]{1,0:T(8,128)(2,1)}, u32[]{:S(2)}, u32[]{:S(2)}) collective-permute-start(bf16[2560,2560]{1,0:T(8,128)(2,1)} %add_convert_fusion.1), channel_id=1, source_target_pairs={{0,1},{1,0},{2,3},{3,2},{4,5},{5,4},{6,7},{7,6}} | collective-permute-start | bytes 39321608 | tf_op jit(solution)/shard_map/ppermute | solution.py:77
  1864.3 228.6 %collective-permute-start.29 = (f32[1024,2560]{1,0:T(8,128)}, f32[1024,2560]{1,0:T(8,128)}, u32[]{:S(2)}, u32[]{:S(2)}) collective-permute-start(f32[1024,2560]{1,0:T(8,128)} %add.372), channel_id=1, source_target_pairs={{0,4},{4,0},{1,5},{5,1},{2,6},{6,2},{3,7},{7,3}} | collective-permute-start | bytes 31457288 | tf_op jit(solution)/shard_map/ppermute | solution.py:77
  1864.8 228.6 %collective-permute-start.27 = (f32[1024,2560]{1,0:T(8,128)}, f32[1024,2560]{1,0:T(8,128)}, u32[]{:S(2)}, u32[]{:S(2)}) collective-permute-start(f32[1024,2560]{1,0:T(8,128)} %convolution_add_fusion.10), channel_id=1, source_target_pairs={{0,2},{2,0},{1,3},{3,1},{4,6},{6,4},{5,7},{7,5}} | collective-permute-start | bytes 31457288 | tf_op jit(solution)/shard_map/ppermute | solution.py:77
  1865.1 116.9 %collective-permute-start.32 = (bf16[2560,2560]{1,0:T(8,128)(2,1)}, bf16[2560,2560]{1,0:T(8,128)(2,1)}, u32[]{:S(2)}, u32[]{:S(2)}) collective-permute-start(bf16[2560,2560]{1,0:T(8,128)(2,1)} %add_convert_fusion.3), channel_id=1, source_target_pairs={{0,1},{1,0},{2,3},{3,2},{4,5},{5,4},{6,7},{7,6}} | collective-permute-start | bytes 39321608 | tf_op jit(solution)/shard_map/ppermute | solution.py:77
  1865.1 451.7 %collective-permute-start.35 = (f32[1024,2560]{1,0:T(8,128)}, f32[1024,2560]{1,0:T(8,128)}, u32[]{:S(2)}, u32[]{:S(2)}) collective-permute-start(f32[1024,2560]{1,0:T(8,128)} %convolution_add_fusion.9), channel_id=1, source_target_pairs={{0,2},{2,0},{1,3},{3,1},{4,6},{6,4},{5,7},{7,5}} | collective-permute-start | bytes 31457288 | tf_op jit(solution)/shard_map/ppermute | solution.py:77
  1964.8 352.8 %collective-permute-start.36 = (f32[1024,2560]{1,0:T(8,128)}, f32[1024,2560]{1,0:T(8,128)}, u32[]{:S(2)}, u32[]{:S(2)}) collective-permute-start(f32[1024,2560]{1,0:T(8,128)} %add.381), channel_id=1, source_target_pairs={{0,4},{4,0},{1,5},{5,1},{2,6},{6,2},{3,7},{7,3}} | collective-permute-start | bytes 31457288 | tf_op jit(solution)/shard_map/ppermute | solution.py:77
  1982.0 616.4 %collective-permute-start.38 = (bf16[1280,5120]{1,0:T(8,128)(2,1)}, bf16[1280,5120]{1,0:T(8,128)(2,1)}, u32[]{:S(2)}, u32[]{:S(2)}) collective-permute-start(bf16[1280,5120]{1,0:T(8,128)(2,1)} %maximum_select_fusion.4), channel_id=1, source_target_pairs={{0,4},{4,0},{1,5},{5,1},{2,6},{6,2},{3,7},{7,3}} | collective-permute-start | bytes 39321608 | tf_op jit(solution)/shard_map/ppermute | solution.py:77
  2342.5 255.1 %collective-permute-start.41 = (f32[2,2560]{1,0:T(2,128)S(1)}, f32[2,2560]{1,0:T(2,128)S(1)}, u32[]{:S(2)}, u32[]{:S(2)}) collective-permute-start(f32[2,2560]{1,0:T(2,128)S(1)} %fusion.7), channel_id=1, source_target_pairs={{0,4},{4,0},{1,5},{5,1},{2,6},{6,2},{3,7},{7,3}} | collective-permute-start | bytes 61448 | tf_op jit(solution)/shard_map/ppermute | solution.py:27
  (67 other events, 3708.5 us)
